TPU v7x, 128 devices: a whole 4x4x4 slice. The times are simulated.
128 devices in a mesh: seq: 32 (over y, x, z_hi), grp: 4 (over z_lo, core).
Axes of the slice: x: 4, y: 4, z: 4 (z_hi: 2, z_lo: 2; z = z_hi * 2 + z_lo), core: 2. Of those that a mesh axis runs over, the one named last changes fastest.
Arguments:
- queries: bfloat16 [32768, 4096], P(('grp', 'seq')), parts along dimension 0, may hold values from -64 to 64
- keys: bfloat16 [32768, 1024], P(('grp', 'seq')), parts along dimension 0, may hold values from -64 to 64
- values: bfloat16 [32768, 1024], P(('grp', 'seq')), parts along dimension 0, may hold values from -6 to 6
- doc_lengths: int32 [24], P('grp'), parts along dimension 0, may hold values from 1 to 32, 64 in all
Outputs:
- attended: bfloat16 [32768, 4096], P(('grp', 'seq')), parts along dimension 0
There are 4 independent parts, one for each index of `grp`. A program takes and returns all parts, laid end to end along the dimension named above; each array names one. Nothing has to cross between parts.
Inputs may be any that keep to these rules, and one draw needn't show every extreme that they name: `doc_lengths`: lengths of the documents in units of 128 tokens, summing to 64.
All inputs are finite; a program needn't handle non-finite values.
Results may differ from a plain program's by a relative error of at most 0.004.
Values may be sent and summed in bfloat16 or wider, within the bound.
A program may use at most 128 MiB of HBM per device.

v0:
```python
import jax
import jax.numpy as jnp
from jax import lax
from jax.sharding import PartitionSpec as P

HEAD_DIM = 128
DOC_UNIT = 128


lowest = -1e30


def doc_starts(doc_lengths):
    lengths = doc_lengths * DOC_UNIT
    return jnp.cumsum(lengths) - lengths


def doc_ids(positions, starts):
    return jnp.sum((positions[:, None] >= starts[None, :]).astype(jnp.int32), axis=1)


def pick_width(total_rows, unit_rows):
    shard_count = total_rows // unit_rows
    most_factor = max(1, 1024 // unit_rows)
    chosen = 1
    for factor in range(1, most_factor + 1):
        if shard_count % factor == 0:
            chosen = factor
    return unit_rows * chosen


def fresh_state(kv_count, group_size, query_rows, head_dim):
    maxima = jnp.full((kv_count, group_size, query_rows), lowest, jnp.float32)
    totals = jnp.zeros((kv_count, group_size, query_rows), jnp.float32)
    accumulated = jnp.zeros((kv_count, group_size, query_rows, head_dim), jnp.float32)
    return (maxima, totals, accumulated)


def update(running, query_rows, query_pos, query_doc, key_part, value_part, key_pos, key_doc):
    scale = query_rows.shape[-1] ** (-0.5)
    needed = (
        (key_pos[0] <= query_pos[-1])
        & (key_doc[-1] >= query_doc[0])
        & (key_doc[0] <= query_doc[-1])
    )

    def compute(current):
        maxima, totals, accumulated = current
        allowed = (key_pos[None, :] <= query_pos[:, None]) & (
            key_doc[None, :] == query_doc[:, None]
        )
        scores = (
            jnp.einsum("qhgd,khd->hgqk", query_rows, key_part, preferred_element_type=jnp.float32)
            * scale
        )
        scores = jnp.where(allowed[None, None], scores, lowest)
        new_max = jnp.maximum(maxima, jnp.max(scores, axis=-1))
        weights = jnp.where(allowed[None, None], jnp.exp(scores - new_max[..., None]), 0.0)
        rescale = jnp.exp(maxima - new_max)
        totals = totals * rescale + jnp.sum(weights, axis=-1)
        mixed = jnp.einsum(
            "hgqk,khd->hgqd",
            weights.astype(jnp.bfloat16),
            value_part,
            preferred_element_type=jnp.float32,
        )
        accumulated = accumulated * rescale[..., None] + mixed
        return (new_max, totals, accumulated)

    def unchanged(current):
        return current

    return lax.cond(needed, compute, unchanged, running)


def sweep_keys(
    running, query_rows, query_pos, query_doc, key_rows, value_rows, key_start, all_docs, unit_rows
):
    total_rows = key_rows.shape[0]
    block_rows = pick_width(total_rows, unit_rows)
    turns = total_rows // block_rows

    def advance(number, current):
        offset = number * block_rows
        key_part = lax.dynamic_slice_in_dim(key_rows, offset, block_rows, 0)
        value_part = lax.dynamic_slice_in_dim(value_rows, offset, block_rows, 0)
        first_key = (key_start + offset).astype(jnp.int32)
        key_pos = first_key + jnp.arange(block_rows, dtype=jnp.int32)
        key_doc = lax.dynamic_slice_in_dim(all_docs, first_key, block_rows, 0)
        return update(
            current, query_rows, query_pos, query_doc, key_part, value_part, key_pos, key_doc
        )

    return lax.fori_loop(0, turns, advance, running)


def finish(running):
    maxima, totals, accumulated = running
    result = accumulated / totals[..., None]
    kv_count, group_size, query_rows, head_dim = result.shape
    return (
        result.transpose(2, 0, 1, 3)
        .reshape(query_rows, kv_count * group_size * head_dim)
        .astype(jnp.bfloat16)
    )


def on_device(queries, keys, values, doc_lengths):
    row_count = queries.shape[0]
    head_dim = HEAD_DIM
    kv_total = keys.shape[1] // head_dim
    heads_total = queries.shape[1] // head_dim
    group_size = heads_total // kv_total
    seq_count = lax.axis_size("seq")
    starts = doc_starts(doc_lengths)
    every_pos = jnp.arange(row_count * seq_count, dtype=jnp.int32)
    all_docs = doc_ids(every_pos, starts)
    heads_dev = heads_total // seq_count
    kv_dev = max(1, heads_dev // group_size)
    repeat_count = max(1, group_size // heads_dev)
    sub_group = heads_dev // kv_dev
    key_send = jnp.repeat(
        keys.reshape(row_count, kv_total, head_dim), repeat_count, axis=1
    ).reshape(row_count, seq_count * kv_dev * head_dim)
    value_send = jnp.repeat(
        values.reshape(row_count, kv_total, head_dim), repeat_count, axis=1
    ).reshape(row_count, seq_count * kv_dev * head_dim)
    all_queries, all_keys, all_values = (
        lax.all_to_all(queries, "seq", split_axis=1, concat_axis=0, tiled=True),
        lax.all_to_all(key_send, "seq", split_axis=1, concat_axis=0, tiled=True),
        lax.all_to_all(value_send, "seq", split_axis=1, concat_axis=0, tiled=True),
    )
    total_rows = all_queries.shape[0]
    all_keys = all_keys.reshape(total_rows, kv_dev, head_dim)
    all_values = all_values.reshape(total_rows, kv_dev, head_dim)
    block_rows = pick_width(total_rows, row_count)
    block_count = total_rows // block_rows
    query_blocks = all_queries.reshape(block_count, block_rows, kv_dev, sub_group, head_dim)

    def attend_block(inputs):
        query_part, number = inputs
        first_query = number * block_rows
        query_pos = first_query + jnp.arange(block_rows, dtype=jnp.int32)
        query_doc = lax.dynamic_slice_in_dim(all_docs, first_query, block_rows, 0)
        running = sweep_keys(
            fresh_state(kv_dev, sub_group, block_rows, head_dim),
            query_part,
            query_pos,
            query_doc,
            all_keys,
            all_values,
            0,
            all_docs,
            row_count,
        )
        return finish(running)

    outputs = lax.map(attend_block, (query_blocks, jnp.arange(block_count, dtype=jnp.int32)))
    outputs = outputs.reshape(total_rows, heads_dev * head_dim)
    return lax.all_to_all(outputs, "seq", split_axis=0, concat_axis=1, tiled=True)


def solution(mesh):
    placed = (P(("grp", "seq"), None), P(("grp", "seq"), None), P(("grp", "seq"), None), P("grp"))
    return jax.shard_map(
        on_device, mesh=mesh, in_specs=placed, out_specs=P(("grp", "seq"), None), check_vma=False
    )
```

profile of v0, /device:TPU:33, one launch (start us, length us, event | category | flops | bytes accessed | tf_op | source)
XLA Modules:
  0.0 670.0 jit_solution(10136841114953952522)
XLA Ops:
  3.1 9.6 %all-to-all-start.1 = ((bf16[256,32,128]{2,0,1:T(8,128)(2,1)}), bf16[256,32,128]{2,0,1:T(8,128)(2,1)}, u32[]{:S(2)}, u32[]{:S(2)}) async-start(bf16[256,32,128]{2,0,1:T(8,128)(2,1)} %bitcast.101), calls=%async_computation.1 | async-start | bytes 4194304 | tf_op jit(solution)/shard_map/all_to_all | solution.py:130
  12.8 29.9 %all-to-all-done.1 = bf16[256,32,128]{2,0,1:T(8,128)(2,1)} async-done(((bf16[256,32,128]{2,0,1:T(8,128)(2,1)}), bf16[256,32,128]{2,0,1:T(8,128)(2,1)}, u32[]{:S(2)}, u32[]{:S(2)}) %all-to-all-start.1) | async-done | bytes 2097184 | tf_op jit(solution)/shard_map/all_to_all | solution.py:130
  51.7 27.2 %all-to-all-done.2 = bf16[256,32,128]{2,0,1:T(8,128)(2,1)} async-done(((bf16[256,32,128]{2,0,1:T(8,128)(2,1)}), bf16[256,32,128]{2,0,1:T(8,128)(2,1)}, u32[]{:S(2)}, u32[]{:S(2)}) %all-to-all-start.2) | async-done | bytes 2097184 | tf_op jit(solution)/shard_map/all_to_all | solution.py:131
  84.4 28.9 %all-to-all-done = bf16[256,32,128]{2,0,1:T(8,128)(2,1)} async-done(((bf16[256,32,128]{2,0,1:T(8,128)(2,1)}), bf16[256,32,128]{2,0,1:T(8,128)(2,1)}, u32[]{:S(2)}, u32[]{:S(2)}) %all-to-all-start) | async-done | bytes 2097184 | tf_op jit(solution)/shard_map/all_to_all | solution.py:129
  113.3 524.1 %while.28 = (s32[]{:T(128)}, bf16[8,1024,128]{2,1,0:T(8,128)(2,1)}, s32[8]{0:T(128)S(1)}, s32[8192]{0:T(1024)S(1)}, bf16[8,1024,1,1,128]{4,1,3,2,0:T(8,128)(2,1)...) while((s32[]{:T(128)}, bf16[8,1024,128]{2,1,0:T(8,128)(2,1)}, ...), condition=%wide.region_9.10_spmd, body=%wide.region_2.9_spmd.sunk | while | flops 560467968 | bytes 16406792 | solution.py:158
  115.7 50.7 %while.29 = (s32[]{:T(128)}, f32[1,1,1024]{2,1,0:T(1,128)S(1)}, f32[1,1,1024]{2,1,0:T(1,128)S(1)}, f32[1,1,1024,128]{3,2,1,0:T(8,128)S(1)}, s32[1024]{0:T(1024)S...) while((s32[]{:T(128)}, f32[1,1,1024]{2,1,0:T(1,128)S(1)}, ...), condition=%wide.region_8.8_spmd, body=%wide.region_3.7_spmd.sunk | while | flops 560204800 | bytes 14546337 | solution.py:94
  121.2 6.6 conditional.2
  169.7 57.3 %while.29 = (s32[]{:T(128)}, f32[1,1,1024]{2,1,0:T(1,128)S(1)}, f32[1,1,1024]{2,1,0:T(1,128)S(1)}, f32[1,1,1024,128]{3,2,1,0:T(8,128)S(1)}, s32[1024]{0:T(1024)S...) while((s32[]{:T(128)}, f32[1,1,1024]{2,1,0:T(1,128)S(1)}, ...), condition=%wide.region_8.8_spmd, body=%wide.region_3.7_spmd.sunk | while | flops 560204800 | bytes 14546337 | solution.py:94
  175.2 6.6 conditional.2
  187.3 6.6 conditional.2
  230.3 57.3 %while.29 = (s32[]{:T(128)}, f32[1,1,1024]{2,1,0:T(1,128)S(1)}, f32[1,1,1024]{2,1,0:T(1,128)S(1)}, f32[1,1,1024,128]{3,2,1,0:T(8,128)S(1)}, s32[1024]{0:T(1024)S...) while((s32[]{:T(128)}, f32[1,1,1024]{2,1,0:T(1,128)S(1)}, ...), condition=%wide.region_8.8_spmd, body=%wide.region_3.7_spmd.sunk | while | flops 560204800 | bytes 14546337 | solution.py:94
  241.3 6.6 conditional.2
  253.4 6.6 conditional.2
  290.8 63.9 %while.29 = (s32[]{:T(128)}, f32[1,1,1024]{2,1,0:T(1,128)S(1)}, f32[1,1,1024]{2,1,0:T(1,128)S(1)}, f32[1,1,1024,128]{3,2,1,0:T(8,128)S(1)}, s32[1024]{0:T(1024)S...) while((s32[]{:T(128)}, f32[1,1,1024]{2,1,0:T(1,128)S(1)}, ...), condition=%wide.region_8.8_spmd, body=%wide.region_3.7_spmd.sunk | while | flops 560204800 | bytes 14546337 | solution.py:94
  313.9 6.6 conditional.2
  326.0 6.6 conditional.2
  358.0 70.5 %while.29 = (s32[]{:T(128)}, f32[1,1,1024]{2,1,0:T(1,128)S(1)}, f32[1,1,1024]{2,1,0:T(1,128)S(1)}, f32[1,1,1024,128]{3,2,1,0:T(8,128)S(1)}, s32[1024]{0:T(1024)S...) while((s32[]{:T(128)}, f32[1,1,1024]{2,1,0:T(1,128)S(1)}, ...), condition=%wide.region_8.8_spmd, body=%wide.region_3.7_spmd.sunk | while | flops 560204800 | bytes 14546337 | solution.py:94
  381.1 6.6 conditional.2
  393.2 6.6 conditional.2
  405.3 6.6 conditional.2
  431.7 77.1 %while.29 = (s32[]{:T(128)}, f32[1,1,1024]{2,1,0:T(1,128)S(1)}, f32[1,1,1024]{2,1,0:T(1,128)S(1)}, f32[1,1,1024,128]{3,2,1,0:T(8,128)S(1)}, s32[1024]{0:T(1024)S...) while((s32[]{:T(128)}, f32[1,1,1024]{2,1,0:T(1,128)S(1)}, ...), condition=%wide.region_8.8_spmd, body=%wide.region_3.7_spmd.sunk | while | flops 560204800 | bytes 14546337 | solution.py:94
  454.8 6.6 conditional.2
  466.9 6.6 conditional.2
  479.1 6.6 conditional.2
  491.2 6.6 conditional.2
  512.1 57.3 %while.29 = (s32[]{:T(128)}, f32[1,1,1024]{2,1,0:T(1,128)S(1)}, f32[1,1,1024]{2,1,0:T(1,128)S(1)}, f32[1,1,1024,128]{3,2,1,0:T(8,128)S(1)}, s32[1024]{0:T(1024)S...) while((s32[]{:T(128)}, f32[1,1,1024]{2,1,0:T(1,128)S(1)}, ...), condition=%wide.region_8.8_spmd, body=%wide.region_3.7_spmd.sunk | while | flops 560204800 | bytes 14546337 | solution.py:94
  545.1 6.6 conditional.2
  557.2 6.6 conditional.2
  572.6 63.9 %while.29 = (s32[]{:T(128)}, f32[1,1,1024]{2,1,0:T(1,128)S(1)}, f32[1,1,1024]{2,1,0:T(1,128)S(1)}, f32[1,1,1024,128]{3,2,1,0:T(8,128)S(1)}, s32[1024]{0:T(1024)S...) while((s32[]{:T(128)}, f32[1,1,1024]{2,1,0:T(1,128)S(1)}, ...), condition=%wide.region_8.8_spmd, body=%wide.region_3.7_spmd.sunk | while | flops 560204800 | bytes 14546337 | solution.py:94
  617.8 6.6 conditional.2
  629.9 6.6 conditional.2
  637.5 24.4 %all_to_all.67 = bf16[32,256,128]{2,1,0:T(8,128)(2,1)} all-to-all(bf16[32,256,128]{2,1,0:T(8,128)(2,1)} %bitcast.107), channel_id=1, replica_groups=mesh['seq'=32,'grp'=4] {'seq'}, dimensions={0} | all-to-all | bytes 4194304 | tf_op jit(solution)/shard_map/all_to_all | solution.py:160
  (583 shorter events, 329.2 us)
Async XLA Ops:
  0.0 49.7 %copy-start = (bf16[256,4096]{1,0:T(8,128)(2,1)S(1)}, bf16[256,4096]{1,0:T(8,128)(2,1)}, u32[]{:S(2)}) copy-start(bf16[256,4096]{1,0:T(8,128)(2,1)} %param.10) | copy-start | bytes 6291460
  0.0 12.7 %copy-start.1 = (bf16[256,1024]{1,0:T(8,128)(2,1)S(1)}, bf16[256,1024]{1,0:T(8,128)(2,1)}, u32[]{:S(2)}) copy-start(bf16[256,1024]{1,0:T(8,128)(2,1)} %param.12) | copy-start | bytes 1572868
  3.1 39.6 %all-to-all-start.1 = ((bf16[256,32,128]{2,0,1:T(8,128)(2,1)}), bf16[256,32,128]{2,0,1:T(8,128)(2,1)}, u32[]{:S(2)}, u32[]{:S(2)}) async-start(bf16[256,32,128]{2,0,1:T(8,128)(2,1)} %bitcast.101), calls=%async_computation.1 | async-start | bytes 4194304 | tf_op jit(solution)/shard_map/all_to_all | solution.py:130
  44.5 34.4 %all-to-all-start.2 = ((bf16[256,32,128]{2,0,1:T(8,128)(2,1)}), bf16[256,32,128]{2,0,1:T(8,128)(2,1)}, u32[]{:S(2)}, u32[]{:S(2)}) async-start(bf16[256,32,128]{2,0,1:T(8,128)(2,1)} %bitcast.102), calls=%async_computation.2 | async-start | bytes 4194304 | tf_op jit(solution)/shard_map/all_to_all | solution.py:131
  49.8 34.3 %copy-start.2 = (s32[6]{0:T(128)S(1)}, s32[6]{0:T(128)}, u32[]{:S(2)}) copy-start(s32[6]{0:T(128)} %param.13) | copy-start | bytes 76
  78.9 34.4 %all-to-all-start = ((bf16[256,32,128]{2,0,1:T(8,128)(2,1)}), bf16[256,32,128]{2,0,1:T(8,128)(2,1)}, u32[]{:S(2)}, u32[]{:S(2)}) async-start(bf16[256,32,128]{2,0,1:T(8,128)(2,1)} %copy_bitcast_fusion), calls=%async_computation | async-start | bytes 4194304 | tf_op jit(solution)/shard_map/all_to_all | solution.py:129
where the time goes:
time: 681 us; the launch traced here: 670 us
  loops' own time  248 us (36%)
  local copies, waits for them, and re-layouts  140 us (21%)
  matrix products  108 us (16%)
  waiting for transfers between devices  86 us (13%)
  other arithmetic  43.7 us (6%)
  blocking collectives  24.4 us (4%)
  starting transfers between devices  20 us (3%)
    another operation x8, loops' own time, sweep_keys(): return lax.fori_loop(0, turns, advance, running)  240 us
    dot_general x22, matrix products, compute(): jnp.einsum('hgqk,khd->hgqd', weights.astype(jnp.bfloat16), value_part, pr...  59.1 us
    dot_general x22, matrix products, compute(): jnp.einsum('qhgd,khd->hgqk', query_rows, key_part, preferred_element_type...  49.1 us
    slice x64, local copies, waits for them, and re-layouts, update(): query_doc[-1]  39.2 us
    slice x64, local copies, waits for them, and re-layouts, update(): query_pos[-1]  38.6 us
    reduce_sum x22, other arithmetic, compute(): totals = totals * rescale + jnp.sum(weights, axis=-1)  35.1 us
    slice x64, local copies, waits for them, and re-layouts, update(): key_pos[0] <= query_pos[-1]  33.3 us
    all_to_all x1, waiting for transfers between devices, on_device(): lax.all_to_all(key_send, 'seq', split_axis=1, concat_axis=0, tiled=True)  29.9 us
  transfers between devices with their start and end apart: 3, of which 3 were waited for; matrix products, arithmetic and copies ran while one was open for 0% of the time, Pallas kernels for 0%

commit v1 on v0

v1 whole, which is shorter than its diff:
```python
import functools

import jax
import jax.numpy as jnp
from jax import lax
from jax.experimental import pallas as pl
from jax.experimental.pallas import tpu as pltpu
from jax.sharding import PartitionSpec as P

DIM = 128
UNIT = 128
ROWS = 256
TOKENS = 8192
DOCS = 6
TILE = 1024
CHUNK = 512
UNITS = 4
VROWS = 136
SCALE = float(DIM**-0.5 * 1.4426950408889634)
FAR = float(2**21)
NEG = -1e30
MESH = pl.DeviceIdType.MESH


def kernel(
    lengths, q_hbm, k_hbm, v_hbm, out_hbm,
    qin, kbuf, vbuf, vt, kext, qfeat, qx, acc, s_scr, p_scr, obuf,
    q_send, q_recv, a_send, a_recv, f_send, f_recv, o_send, o_recv,
):
    me = lax.axis_index("seq")
    y, x, z = me // 8, (me // 2) % 4, me % 2
    xh, xl = x // 2, x % 2
    mine = 2 * y + xl
    x_mate = y * 8 + (3 - x) * 2 + z
    z_mate = y * 8 + x * 2 + 1 - z

    def device(j):
        return (j // 2) * 8 + (2 * xh + j % 2) * 2 + z

    def head(j):
        return 2 * (j // 2) + (j % 2 + xh) % 2

    def block(j, half, side):
        number = (j // 2) * 8 + (2 * half + j % 2) * 2 + side
        return pl.ds(pl.multiple_of(number * ROWS, ROWS), ROWS)

    def cols(start, size):
        return pl.ds(pl.multiple_of(start, DIM), size)

    def remote(src, dst, send, recv, to):
        return pltpu.make_async_remote_copy(
            src_ref=src, dst_ref=dst, send_sem=send, recv_sem=recv,
            device_id={"seq": to}, device_id_type=MESH,
        )

    def kv_in(which, j_from, j_to):
        hbm, buf = ((k_hbm, kbuf), (v_hbm, vbuf))[which]
        return (
            hbm.at[:, cols(head(j_to) * DIM, DIM)],
            buf.at[block(j_from, xh, z), :],
        )

    def q_in(ph, j_from, j_to):
        return (
            q_hbm.at[:, cols(head(j_to) * 4 * DIM + ph * 2 * DIM, 2 * DIM)],
            qin.at[ph, j_from],
        )

    def kv_copy(which, j_to):
        src, dst = kv_in(which, mine, j_to)
        return remote(src, dst, a_send.at[which, j_to], a_recv.at[which, mine], device(j_to))

    def q_copy(ph, j_to):
        src, dst = q_in(ph, mine, j_to)
        return remote(src, dst, q_send.at[ph, j_to], q_recv.at[ph, mine], device(j_to))

    def kv_arrived(which, j):
        src, dst = kv_in(which, j, mine)
        return remote(src, dst, a_send.at[which, j], a_recv.at[which, j], device(j))

    def q_arrived(ph, j):
        src, dst = q_in(ph, j, mine)
        return remote(src, dst, q_send.at[ph, j], q_recv.at[ph, j], device(j))

    def forward(kind, j, sending):
        buf = kbuf if kind in (0, 1, 4) else vbuf
        to = z_mate if kind in (0, 2, 5) else x_mate
        half, side = xh, z
        if sending:
            if kind == 4:
                side = 1 - z
            if kind == 5:
                half = 1 - xh
        else:
            if kind in (0, 2):
                side = 1 - z
            elif kind in (1, 3):
                half = 1 - xh
            else:
                half, side = 1 - xh, 1 - z
        rows = buf.at[block(j, half, side), :]
        return remote(rows, rows, f_send.at[kind, j], f_recv.at[kind, j], to)

    barrier = pltpu.get_barrier_semaphore()

    def greet(o, c):
        pl.semaphore_signal(
            barrier, inc=1, device_id={"seq": device((mine + o) % 8)}, device_id_type=MESH
        )
        return c

    own = []
    for which in range(2):
        src, dst = kv_in(which, mine, mine)
        own.append(pltpu.make_async_copy(src, dst, a_recv.at[which, mine]))
    for ph in range(2):
        src, dst = q_in(ph, mine, mine)
        own.append(pltpu.make_async_copy(src, dst, q_recv.at[ph, mine]))
    for copy in own:
        copy.start()
    lax.fori_loop(1, 8, greet, 0)
    pl.semaphore_signal(barrier, inc=1, device_id={"seq": x_mate}, device_id_type=MESH)
    pl.semaphore_signal(barrier, inc=1, device_id={"seq": z_mate}, device_id_type=MESH)
    pl.semaphore_wait(barrier, 9)

    def send_kv(o, c):
        for which in range(2):
            kv_copy(which, (mine + o) % 8).start()
        return c

    def send_q(ph):
        def go(o, c):
            q_copy(ph, (mine + o) % 8).start()
            return c

        lax.fori_loop(1, 8, go, 0)

    lax.fori_loop(1, 8, send_kv, 0)
    send_q(0)
    send_q(1)

    starts, total = [], jnp.int32(0)
    for d in range(DOCS):
        starts.append(total)
        total = total + lengths[d] * UNIT
    ends = starts[1:] + [total]

    lane = lax.broadcasted_iota(jnp.int32, (1, DIM), 1)
    low, high = jnp.zeros((1, DIM), jnp.int32), jnp.full((1, DIM), TOKENS, jnp.int32)
    for d in range(DOCS):
        low, high = jnp.where(lane == d, starts[d], low), jnp.where(lane == d, ends[d], high)

    def key_features(i, c):
        first = pl.multiple_of(i * ROWS, ROWS)
        token = first + lax.broadcasted_iota(jnp.int32, (ROWS, DIM), 0)
        inside = (token >= low) & (token < high)
        kext[pl.ds(first, ROWS), :] = jnp.where(inside, 0.0, -FAR).astype(jnp.bfloat16)
        return c

    feature = lax.broadcasted_iota(jnp.int32, (DIM, ROWS), 0)
    low_row, high_row = jnp.full((DIM, ROWS), TOKENS, jnp.int32), jnp.zeros((DIM, ROWS), jnp.int32)
    for d in range(DOCS):
        low_row = jnp.where(feature == d, starts[d], low_row)
        high_row = jnp.where(feature == d, ends[d], high_row)

    def query_features(j, c):
        first = ((j // 2) * 8 + (2 * xh + j % 2) * 2 + z) * ROWS
        token = first + lax.broadcasted_iota(jnp.int32, (DIM, ROWS), 1)
        inside = (token >= low_row) & (token < high_row)
        qfeat[j] = jnp.where(inside, 1.0, 0.0).astype(jnp.bfloat16)
        return c

    ones = lax.broadcasted_iota(jnp.int32, (VROWS - DIM, ROWS), 0) == 0
    ones = jnp.where(ones, 1.0, 0.0).astype(jnp.bfloat16)

    def hop1(r):
        for j in (2 * r, 2 * r + 1):
            kv_arrived(0, j).wait_recv()
            forward(0, j, True).start()
            forward(1, j, True).start()
            kv_arrived(1, j).wait_recv()
            forward(2, j, True).start()
            forward(3, j, True).start()

    def relay(r):
        for j in (2 * r, 2 * r + 1):
            forward(0, j, False).wait_recv()
            forward(4, j, True).start()
            forward(3, j, False).wait_recv()
            forward(5, j, True).start()

    hop1(0)
    hop1(1)
    lax.fori_loop(0, TOKENS // ROWS, key_features, 0)
    relay(0)
    hop1(2)
    lax.fori_loop(0, 8, query_features, 0)
    relay(1)
    hop1(3)

    def receive_row(r):
        for j in (2 * r, 2 * r + 1):
            for kind in (1, 2, 4, 5):
                forward(kind, j, False).wait_recv()

        def turn(i, c):
            rows = pl.ds(pl.multiple_of((8 * r + i) * ROWS, ROWS), ROWS)
            vt[:DIM, rows] = vbuf[rows, :].T
            vt[DIM:, rows] = ones
            return c

        lax.fori_loop(0, 8, turn, 0)

    def scores(t, u, c, mx, qoff=None):
        rows = pl.ds(pl.multiple_of(t * TILE + c * CHUNK, CHUNK), CHUNK)
        left = jnp.concatenate([kbuf[rows, :], kext[rows, :]], axis=1)
        s = jnp.dot(left, qx[u], preferred_element_type=jnp.float32)
        if qoff is not None:
            off = c * CHUNK + lax.broadcasted_iota(jnp.int32, (CHUNK, ROWS), 0)
            s = jnp.where(off <= qoff, s, NEG)
        s_scr[u, c * CHUNK : (c + 1) * CHUNK, :] = s
        part = jnp.max(s.reshape(CHUNK // 8, 8, ROWS), axis=0)
        return part if mx is None else jnp.maximum(mx, part)

    def weigh(u, c, mc):
        s = s_scr[u, c * CHUNK : (c + 1) * CHUNK, :]
        p_scr[u, c * CHUNK : (c + 1) * CHUNK, :] = jnp.exp2(s * SCALE - mc).astype(jnp.bfloat16)

    def row_step(step, carry):
        ph, r = step // 4, step % 4

        @pl.when(ph == 0)
        def _():
            @pl.when((r == 1) | (r == 2))
            def _():
                relay(r + 1)

            receive_row(r)

        for k in range(2):
            q_arrived(ph, 2 * r + k).wait_recv()
        for u in range(UNITS):
            j = 2 * r + u // 2
            qx[u, :DIM, :] = qin[ph, j, :, (u % 2) * DIM : (u % 2 + 1) * DIM].T
            qx[u, DIM:, :] = qfeat[j]

        last = 2 * r + xh
        lanes = z * ROWS + lax.broadcasted_iota(jnp.int32, (1, ROWS), 1)

        mx = None
        for c in range(TILE // CHUNK):
            mx = scores(last, 0, c, mx, lanes)
        top = []
        for u in range(UNITS):
            m = jnp.max(mx, axis=0, keepdims=True)
            mc = m * SCALE
            mx = None
            for c in range(TILE // CHUNK):
                if u < UNITS - 1:
                    mx = scores(last, u + 1, c, mx, lanes + ((u + 1) // 2) * 512)
                else:
                    mx = scores(jnp.maximum(last - 1, 0), 0, c, mx)
                weigh(u, c, mc)
            keys = pl.ds(pl.multiple_of(last * TILE, TILE), TILE)
            acc[u] = jnp.dot(vt[:, keys], p_scr[u], preferred_element_type=jnp.float32)
            top.append(m)

        def back(i, carry):
            tops, mx = carry
            tops = list(tops)
            t = last - 1 - i
            keys = pl.ds(pl.multiple_of(t * TILE, TILE), TILE)
            for u in range(UNITS):
                m = jnp.maximum(tops[u], jnp.max(mx, axis=0, keepdims=True))
                drop = jnp.exp2((tops[u] - m) * SCALE)
                mc = m * SCALE
                mx = None
                for c in range(TILE // CHUNK):
                    if u < UNITS - 1:
                        mx = scores(t, u + 1, c, mx)
                    else:
                        mx = scores(jnp.maximum(t - 1, 0), 0, c, mx)
                    weigh(u, c, mc)
                acc[u] = acc[u] * drop + jnp.dot(
                    vt[:, keys], p_scr[u], preferred_element_type=jnp.float32
                )
                tops[u] = m
            return tuple(tops), mx

        lax.fori_loop(0, jnp.minimum(last, 4), back, (tuple(top), mx))

        for k in range(2):
            j = 2 * r + k
            for n in range(2):
                u = 2 * k + n
                o = acc[u, :DIM, :] * (1.0 / acc[u, DIM : DIM + 1, :])
                obuf[ph, j, :, n * DIM : (n + 1) * DIM] = o.T.astype(jnp.bfloat16)

            @pl.when(j == mine)
            def _():
                local_out(ph).start()

            @pl.when(j != mine)
            def _():
                out_copy(ph, j).start()
        return carry

    def place_out(ph, j):
        return out_hbm.at[:, cols(head(j) * 4 * DIM + ph * 2 * DIM, 2 * DIM)]

    def local_out(ph):
        return pltpu.make_async_copy(obuf.at[ph, mine], place_out(ph, mine), o_send.at[ph, mine])

    def out_copy(ph, j):
        return remote(
            obuf.at[ph, j], place_out(ph, mine), o_send.at[ph, j], o_recv.at[ph, mine], device(j)
        )

    def out_arrived(ph, j):
        return remote(
            obuf.at[ph, j], place_out(ph, j), o_send.at[ph, j], o_recv.at[ph, j], device(j)
        )

    lax.fori_loop(0, 8, row_step, 0)

    for ph in range(2):
        local_out(ph).wait()

    def drain(o, c):
        j = (mine + o) % 8
        for i in range(2):
            kv_copy(i, j).wait_send()
            q_copy(i, j).wait_send()
            out_copy(i, j).wait_send()
            out_arrived(i, j).wait_recv()
        return c

    lax.fori_loop(1, 8, drain, 0)

    def drain_forward(j, c):
        for kind in range(6):
            forward(kind, j, True).wait_send()
        return c

    lax.fori_loop(0, 8, drain_forward, 0)


def on_device(queries, keys, values, doc_lengths):
    bf16, f32 = jnp.bfloat16, jnp.float32
    dma = pltpu.SemaphoreType.DMA
    hbm = pl.BlockSpec(memory_space=pl.ANY)
    return pl.pallas_call(
        kernel,
        out_shape=jax.ShapeDtypeStruct(queries.shape, bf16),
        in_specs=[pl.BlockSpec(memory_space=pltpu.SMEM), hbm, hbm, hbm],
        out_specs=hbm,
        scratch_shapes=[
            pltpu.VMEM((2, 8, ROWS, 2 * DIM), bf16),
            pltpu.VMEM((TOKENS, DIM), bf16),
            pltpu.VMEM((TOKENS, DIM), bf16),
            pltpu.VMEM((VROWS, TOKENS), bf16),
            pltpu.VMEM((TOKENS, DIM), bf16),
            pltpu.VMEM((8, DIM, ROWS), bf16),
            pltpu.VMEM((UNITS, 2 * DIM, ROWS), bf16),
            pltpu.VMEM((UNITS, VROWS, ROWS), f32),
            pltpu.VMEM((UNITS, TILE, ROWS), f32),
            pltpu.VMEM((UNITS, TILE, ROWS), bf16),
            pltpu.VMEM((2, 8, ROWS, 2 * DIM), bf16),
            dma((2, 8)), dma((2, 8)), dma((2, 8)), dma((2, 8)),
            dma((6, 8)), dma((6, 8)), dma((2, 8)), dma((2, 8)),
        ],
        compiler_params=pltpu.CompilerParams(
            collective_id=0, has_side_effects=True, vmem_limit_bytes=48 << 20
        ),
    )(doc_lengths, queries, keys, values)


def solution(mesh):
    placed = (P(("grp", "seq"), None), P(("grp", "seq"), None), P(("grp", "seq"), None), P("grp"))
    return jax.shard_map(
        on_device, mesh=mesh, in_specs=placed, out_specs=P(("grp", "seq"), None), check_vma=False
    )
```

time: 681 us -> 110 us (0.16)
  the two profiles are of different devices: /device:TPU:33 before, /device:TPU:30 now
where the time goes in v1:
time: 110 us
  Pallas kernels  105 us (95%)
  local copies, waits for them, and re-layouts  5.65 us (5%)
    pallas_call x1, Pallas kernels, on_device(): pl.pallas_call(kernel, out_shape=jax.ShapeDtypeStruct(queries.shape, bf16...  105 us
    unnamed x9, local copies, waits for them, and re-layouts  5.65 us

profile of v1, /device:TPU:30, one launch (start us, length us, event | category | flops | bytes accessed | tf_op | source)
XLA Modules:
  0.0 110.2 jit_solution(16581696497974306903)
XLA Ops:
  0.0 0.0 copy-start
  0.0 1.6 %copy-done = bf16[256,4096]{1,0:T(8,128)(2,1)S(1)} copy-done((bf16[256,4096]{1,0:T(8,128)(2,1)S(1)}, bf16[256,4096]{1,0:T(8,128)(2,1)}, u32[]{:S(2)}) %copy-start) | copy-done | bytes 2097176
  1.6 0.0 copy-start.1
  1.6 1.0 copy-done.1
  2.6 0.0 copy-start.2
  2.6 1.0 copy-done.2
  3.7 0.0 copy-start.3
  3.7 0.7 copy-done.3
  4.3 104.5 %shard_map.46 = bf16[256,4096]{1,0:T(8,128)(2,1)S(1)} custom-call(s32[6]{0:T(128)S(1)} %copy-done.3, bf16[256,4096]{1,0:T(8,128)(2,1)S(1)} %copy-done, bf16[256,1024]{1,0:T(8,128)(2,1)S(1)} %copy-done.1, bf16[256,1024]{1,0:T(8,128)(2,1)S(1)} %copy-done.2), custom_call_target="tpu_custom_call" | custom-call | tf_op jit(solution)/shard_map/pallas_call | solution.py:352
  108.9 1.3 %copy.6 = bf16[256,4096]{1,0:T(8,128)(2,1)} copy(bf16[256,4096]{1,0:T(8,128)(2,1)S(1)} %shard_map.46) | data formatting | bytes 4194304
Async XLA Ops:
  0.0 1.6 %copy-start = (bf16[256,4096]{1,0:T(8,128)(2,1)S(1)}, bf16[256,4096]{1,0:T(8,128)(2,1)}, u32[]{:S(2)}) copy-start(bf16[256,4096]{1,0:T(8,128)(2,1)} %q_hbm.1) | copy-start | bytes 6291460
  1.6 1.0 copy-start.1
  2.6 1.0 copy-start.2
  3.7 0.7 copy-start.3

commit v2 on v1

v2 whole, which is shorter than its diff:
```python
import functools

import jax
import jax.numpy as jnp
from jax import lax
from jax.experimental import pallas as pl
from jax.experimental.pallas import tpu as pltpu
from jax.sharding import PartitionSpec as P

DIM = 128
UNIT = 128
ROWS = 256
TOKENS = 8192
DOCS = 6
TILE = 1024
CHUNK = 512
UNITS = 8
VROWS = 136
SCALE = float(DIM**-0.5 * 1.4426950408889634)
FAR = float(2**21)
NEG = -1e30
MESH = pl.DeviceIdType.MESH


def digits(numbers):
    return sum(n * 4**i for i, n in enumerate(numbers))


ITEMS = (
    ((0, 0), (3, 3), (3, 2), (2, 2), (3, 1), (2, 1), (2, 0), (1, 1), (1, 0)),
    ((1, 1), (1, 0), (0, 0), (3, 3), (3, 2), (3, 1), (2, 2), (2, 1), (2, 0)),
    ((2, 2), (2, 1), (1, 1), (2, 0), (1, 0), (0, 0), (3, 3), (3, 2), (3, 1)),
    ((3, 3), (3, 2), (2, 2), (3, 1), (2, 1), (1, 1), (2, 0), (1, 0), (0, 0)),
)
THIRD, FOURTH = (2, 3, 3, 3), (4, 4, 6, 6)


def by_y(y, values):
    return jnp.where(
        y < 2, jnp.where(y == 0, values[0], values[1]), jnp.where(y == 2, values[2], values[3])
    )


def kernel(
    lengths, q_hbm, k_hbm, v_hbm, out_hbm,
    qin, kbuf, vbuf, vt, kext, qx, acc, m_scr, mx_scr, s_scr, p_scr, obuf,
    q_send, q_recv, a_send, a_recv, f_send, f_recv, o_send, o_recv,
):
    me = lax.axis_index("seq")
    y, x, z = me // 8, (me // 2) % 4, me % 2
    xh, xl = x // 2, x % 2
    mine = 2 * y + xl
    x_mate = y * 8 + (3 - x) * 2 + z
    z_mate = y * 8 + x * 2 + 1 - z
    xz_mate = y * 8 + (3 - x) * 2 + 1 - z

    def device(j):
        return (j // 2) * 8 + (2 * xh + j % 2) * 2 + z

    def head(j):
        return 2 * (j // 2) + (j % 2 + xh) % 2

    def block(j, half, side):
        number = (j // 2) * 8 + (2 * half + j % 2) * 2 + side
        return pl.ds(pl.multiple_of(number * ROWS, ROWS), ROWS)

    def cols(start, size):
        return pl.ds(pl.multiple_of(start, DIM), size)

    def remote(src, dst, send, recv, to):
        return pltpu.make_async_remote_copy(
            src_ref=src, dst_ref=dst, send_sem=send, recv_sem=recv,
            device_id={"seq": to}, device_id_type=MESH,
        )

    def kv_in(which, j_from, j_to):
        hbm, buf = ((k_hbm, kbuf), (v_hbm, vbuf))[which]
        return hbm.at[:, cols(head(j_to) * DIM, DIM)], buf.at[block(j_from, xh, z), :]

    def q_in(j_from, j_to):
        return q_hbm.at[:, cols(head(j_to) * 4 * DIM, 4 * DIM)], qin.at[j_from]

    def kv_copy(which, j_to):
        src, dst = kv_in(which, mine, j_to)
        return remote(src, dst, a_send.at[which, j_to], a_recv.at[which, mine], device(j_to))

    def q_copy(j_to):
        src, dst = q_in(mine, j_to)
        return remote(src, dst, q_send.at[j_to], q_recv.at[mine], device(j_to))

    def kv_arrived(which, j):
        src, dst = kv_in(which, j, mine)
        return remote(src, dst, a_send.at[which, j], a_recv.at[which, j], device(j))

    def q_arrived(j):
        src, dst = q_in(j, mine)
        return remote(src, dst, q_send.at[j], q_recv.at[j], device(j))

    def forward(kind, j, sending):
        buf = (kbuf, vbuf)[kind % 2]
        half, side = xh, z
        if not sending and kind // 2 != 1:
            half = 1 - xh
        if not sending and kind // 2 != 0:
            side = 1 - z
        rows = buf.at[block(j, half, side), :]
        to = (x_mate, z_mate, xz_mate)[kind // 2]
        return remote(rows, rows, f_send.at[kind, j], f_recv.at[kind, j], to)

    barrier = pltpu.get_barrier_semaphore()

    def greet(o, c):
        pl.semaphore_signal(
            barrier, inc=1, device_id={"seq": device((mine + o) % 8)}, device_id_type=MESH
        )
        return c

    lax.fori_loop(1, 8, greet, 0)
    for mate in (x_mate, z_mate, xz_mate):
        pl.semaphore_signal(barrier, inc=1, device_id={"seq": mate}, device_id_type=MESH)
    for which in range(2):
        src, dst = kv_in(which, mine, mine)
        pltpu.make_async_copy(src, dst, a_recv.at[which, mine]).start()
    src, dst = q_in(mine, mine)
    pltpu.make_async_copy(src, dst, q_recv.at[mine]).start()
    pl.semaphore_wait(barrier, 10)

    others = [[2 * ((y + dy) % 4) + (xl + dx) % 2 for dx in range(2)] for dy in range(4)]
    others[0] = others[0][1:]

    def send_kv(dy):
        for j in others[dy]:
            kv_copy(0, j).start()
            kv_copy(1, j).start()

    def send_q(dy):
        for j in others[dy]:
            q_copy(j).start()

    send_kv(0)
    send_kv(1)
    send_kv(2)

    def key_row(i):
        return (y + 4 - i) % 4

    def pass_on(i):
        row = key_row(i)
        for k in range(2):
            j = 2 * row + (xl + k) % 2
            for which in range(2):
                kv_arrived(which, j).wait_recv()
                for mate in (2, 0, 1):
                    forward(2 * mate + which, j, True).start()

    def receive(i):
        row = key_row(i)
        for k in range(2):
            for kind in range(6):
                forward(kind, 2 * row + k, False).wait_recv()

        def turn(n, c):
            rows = pl.ds(pl.multiple_of((8 * row + n) * ROWS, ROWS), ROWS)
            vt[:DIM, rows] = vbuf[rows, :].T
            return c

        lax.fori_loop(0, 8, turn, 0)

    pass_on(0)
    send_q(0)
    send_q(1)
    send_kv(3)

    starts, total = [], jnp.int32(0)
    for d in range(DOCS):
        starts.append(total)
        total = total + lengths[d] * UNIT
    ends = starts[1:] + [total]

    lane = lax.broadcasted_iota(jnp.int32, (1, DIM), 1)
    low, high = jnp.zeros((1, DIM), jnp.int32), jnp.full((1, DIM), TOKENS, jnp.int32)
    for d in range(DOCS):
        low, high = jnp.where(lane == d, starts[d], low), jnp.where(lane == d, ends[d], high)

    def key_features(i, c):
        first = pl.multiple_of(i * ROWS, ROWS)
        token = first + lax.broadcasted_iota(jnp.int32, (ROWS, DIM), 0)
        inside = (token >= low) & (token < high)
        kext[pl.ds(first, ROWS), :] = jnp.where(inside, 0.0, -FAR).astype(jnp.bfloat16)
        return c

    lax.fori_loop(0, TOKENS // ROWS, key_features, 0)
    feature = lax.broadcasted_iota(jnp.int32, (DIM, ROWS), 0)
    low_row, high_row = jnp.full((DIM, ROWS), TOKENS, jnp.int32), jnp.zeros((DIM, ROWS), jnp.int32)
    for d in range(DOCS):
        low_row = jnp.where(feature == d, starts[d], low_row)
        high_row = jnp.where(feature == d, ends[d], high_row)

    def query_features(j, c):
        first = ((j // 2) * 8 + (2 * xh + j % 2) * 2 + z) * ROWS
        token = first + lax.broadcasted_iota(jnp.int32, (DIM, ROWS), 1)
        inside = (token >= low_row) & (token < high_row)
        marks = jnp.where(inside, 1.0, 0.0).astype(jnp.bfloat16)
        for n in range(4):
            qx[j // 2, (j % 2) * 4 + n, DIM:, :] = marks
        return c

    lax.fori_loop(0, 8, query_features, 0)
    first_row = lax.broadcasted_iota(jnp.int32, (VROWS - DIM, TOKENS), 0) == 0
    vt[DIM:, :] = jnp.where(first_row, 1.0, 0.0).astype(jnp.bfloat16)

    pass_on(1)
    pass_on(2)
    send_q(2)
    send_q(3)
    receive(0)

    def scores(r, t, u, c, mx, qoff=None):
        rows = pl.ds(pl.multiple_of(t * TILE + c * CHUNK, CHUNK), CHUNK)
        left = jnp.concatenate([kbuf[rows, :], kext[rows, :]], axis=1)
        s = jnp.dot(left, qx[r, u], preferred_element_type=jnp.float32)
        if qoff is not None:
            off = lax.broadcasted_iota(jnp.int32, (CHUNK, ROWS), 0)
            s = jnp.where(off <= qoff, s, NEG)
        s_scr[u, c * CHUNK : (c + 1) * CHUNK, :] = s
        part = jnp.max(s.reshape(CHUNK // 8, 8, ROWS), axis=0)
        return part if mx is None else jnp.maximum(mx, part)

    def weigh(u, c, mc):
        s = s_scr[u, c * CHUNK : (c + 1) * CHUNK, :]
        p = jnp.exp2(s * SCALE - mc).astype(jnp.bfloat16)
        p_scr[u, c * CHUNK : (c + 1) * CHUNK, :] = p

    lanes = z * ROWS + lax.broadcasted_iota(jnp.int32, (1, ROWS), 1)

    def own_tile(r):
        last = 2 * r + xh
        for k in range(2):
            q_arrived(2 * r + k).wait_recv()
            for n in range(4):
                qx[r, 4 * k + n, :DIM, :] = qin[2 * r + k, :, n * DIM : (n + 1) * DIM].T
        mx = scores(r, last, 0, 0, None, lanes)
        for u in range(UNITS):
            m = jnp.max(mx, axis=0, keepdims=True)
            mc = m * SCALE
            mx = None
            for c in range(TILE // CHUNK):
                if u == UNITS - 1:
                    mx = scores(r, 2 * r, 0, c, mx)
                elif c <= (u + 1) // 4:
                    limit = lanes if c == (u + 1) // 4 else None
                    mx = scores(r, last, u + 1, c, mx, limit)
                if c <= u // 4:
                    weigh(u, c, mc)
            size = (u // 4 + 1) * CHUNK
            keys = pl.ds(pl.multiple_of(last * TILE, TILE), size)
            acc[r, u] = jnp.dot(vt[:, keys], p_scr[u, :size], preferred_element_type=jnp.float32)
            m_scr[r, u : u + 1, :] = m
        mx_scr[...] = mx

    def back(r, t, size, mx=None):
        parts = size // CHUNK
        if mx is None:
            for c in range(parts):
                mx = scores(r, t, 0, c, mx)
        keys = pl.ds(pl.multiple_of(t * TILE, TILE), size)
        for u in range(UNITS):
            old = m_scr[r, u : u + 1, :]
            m = jnp.maximum(old, jnp.max(mx, axis=0, keepdims=True))
            drop = jnp.exp2((old - m) * SCALE)
            mc = m * SCALE
            mx = None
            for c in range(parts):
                weigh(u, c, mc)
                if u < UNITS - 1:
                    mx = scores(r, t, u + 1, c, mx)
            acc[r, u] = acc[r, u] * drop + jnp.dot(
                vt[:, keys], p_scr[u, :size], preferred_element_type=jnp.float32
            )
            m_scr[r, u : u + 1, :] = m

    def place_out(j):
        return out_hbm.at[:, cols(head(j) * 4 * DIM, 4 * DIM)]

    def local_out():
        return pltpu.make_async_copy(obuf.at[mine], place_out(mine), o_send.at[mine])

    def out_copy(j):
        return remote(obuf.at[j], place_out(mine), o_send.at[j], o_recv.at[mine], device(j))

    def out_arrived(j):
        return remote(obuf.at[j], place_out(j), o_send.at[j], o_recv.at[j], device(j))

    def finish(r):
        for k in range(2):
            j = 2 * r + k
            for n in range(4):
                u = 4 * k + n
                o = acc[r, u, :DIM, :] * (1.0 / acc[r, u, DIM : DIM + 1, :])
                obuf[j, :, n * DIM : (n + 1) * DIM] = o.astype(jnp.bfloat16).T

            @pl.when(j == mine)
            def _():
                local_out().start()

            @pl.when(j != mine)
            def _():
                out_copy(j).start()

    def item(step, codes):
        r, kr = codes[0] % 4, codes[1] % 4

        @pl.when(step == 1)
        def _():
            pass_on(3)
            receive(1)

        @pl.when(step == by_y(y, THIRD))
        def _():
            receive(2)

        @pl.when(step == by_y(y, FOURTH))
        def _():
            receive(3)

        @pl.when(r == kr)
        def _():
            own_tile(r)

            @pl.when(xh == 1)
            def _():
                back(r, 2 * r, TILE, mx_scr[...])

        @pl.when((kr == r - 1) | ((kr == r - 2) & (xh == 0)))
        def _():
            back(r, 2 * kr, 2 * TILE)

        @pl.when((kr == r - 2) & (xh == 1))
        def _():
            back(r, 2 * kr + 1, TILE)

        @pl.when(kr == jnp.maximum(r - 2, 0))
        def _():
            finish(r)

        return codes[0] // 4, codes[1] // 4

    rows = by_y(y, [digits([i[0] for i in items]) for items in ITEMS])
    keys = by_y(y, [digits([i[1] for i in items]) for items in ITEMS])
    lax.fori_loop(0, 9, item, (rows, keys))

    local_out().wait()

    def drain(o, c):
        j = (mine + o) % 8
        for which in range(2):
            kv_copy(which, j).wait_send()
        q_copy(j).wait_send()
        out_copy(j).wait_send()
        out_arrived(j).wait_recv()
        return c

    lax.fori_loop(1, 8, drain, 0)

    def drain_forward(j, c):
        for kind in range(6):
            forward(kind, j, True).wait_send()
        return c

    lax.fori_loop(0, 8, drain_forward, 0)


def on_device(queries, keys, values, doc_lengths):
    bf16, f32 = jnp.bfloat16, jnp.float32
    dma = pltpu.SemaphoreType.DMA
    hbm = pl.BlockSpec(memory_space=pltpu.HBM)
    return pl.pallas_call(
        kernel,
        out_shape=jax.ShapeDtypeStruct(queries.shape, bf16),
        in_specs=[pl.BlockSpec(memory_space=pltpu.SMEM), hbm, hbm, hbm],
        out_specs=pl.BlockSpec(memory_space=pl.ANY),
        scratch_shapes=[
            pltpu.VMEM((8, ROWS, 4 * DIM), bf16),
            pltpu.VMEM((TOKENS, DIM), bf16),
            pltpu.VMEM((TOKENS, DIM), bf16),
            pltpu.VMEM((VROWS, TOKENS), bf16),
            pltpu.VMEM((TOKENS, DIM), bf16),
            pltpu.VMEM((4, UNITS, 2 * DIM, ROWS), bf16),
            pltpu.VMEM((4, UNITS, VROWS, ROWS), f32),
            pltpu.VMEM((4, UNITS, ROWS), f32),
            pltpu.VMEM((8, ROWS), f32),
            pltpu.VMEM((UNITS, 2 * TILE, ROWS), f32),
            pltpu.VMEM((UNITS, 2 * TILE, ROWS), bf16),
            pltpu.VMEM((8, ROWS, 4 * DIM), bf16),
            dma((8,)), dma((8,)), dma((2, 8)), dma((2, 8)),
            dma((6, 8)), dma((6, 8)), dma((8,)), dma((8,)),
        ],
        compiler_params=pltpu.CompilerParams(
            collective_id=0, has_side_effects=True, vmem_limit_bytes=67043328
        ),
    )(doc_lengths, queries, keys, values)


def solution(mesh):
    placed = (P(("grp", "seq"), None), P(("grp", "seq"), None), P(("grp", "seq"), None), P("grp"))
    return jax.shard_map(
        on_device, mesh=mesh, in_specs=placed, out_specs=P(("grp", "seq"), None), check_vma=False
    )
```

time: 110 us -> 99 us (0.900)
  the two profiles are of different devices: /device:TPU:30 before, /device:TPU:17 now
where the time goes in v2:
time: 99 us; the launch traced here: 98.7 us
  Pallas kernels  95.6 us (97%)
  local copies, waits for them, and re-layouts  3.13 us (3%)
    pallas_call x1, Pallas kernels, on_device(): pl.pallas_call(kernel, out_shape=jax.ShapeDtypeStruct(queries.shape, bf16...  95.6 us
    unnamed x1, local copies, waits for them, and re-layouts  3.13 us

profile of v2, /device:TPU:17, one launch (start us, length us, event | category | flops | bytes accessed | tf_op | source)
XLA Modules:
  0.0 98.7 jit_solution(9149875175208740116)
XLA Ops:
  0.0 95.6 %shard_map.46 = bf16[256,4096]{1,0:T(8,128)(2,1)} custom-call(s32[6]{0:T(128)} %lengths.1, bf16[256,4096]{1,0:T(8,128)(2,1)} %q_hbm.1, bf16[256,1024]{1,0:T(8,128)(2,1)} %k_hbm.1, bf16[256,1024]{1,0:T(8,128)(2,1)} %v_hbm.1), custom_call_target="tpu_custom_call" | custom-call | tf_op jit(solution)/shard_map/pallas_call | solution.py:377
  95.6 3.1 %copy.6 = bf16[256,4096]{1,0:T(8,128)(2,1)} copy(bf16[256,4096]{1,0:T(8,128)(2,1)} %shard_map.46) | data formatting | bytes 4194304

commit v3 on v2

--- a/solution.py
+++ b/solution.py
@@ -27,12 +27,12 @@
 
 
 ITEMS = (
-    ((0, 0), (3, 3), (3, 2), (2, 2), (3, 1), (2, 1), (2, 0), (1, 1), (1, 0)),
+    ((0, 0), (1, 1), (1, 0), (2, 2), (2, 1), (2, 0), (3, 3), (3, 2), (3, 1)),
     ((1, 1), (1, 0), (0, 0), (3, 3), (3, 2), (3, 1), (2, 2), (2, 1), (2, 0)),
     ((2, 2), (2, 1), (1, 1), (2, 0), (1, 0), (0, 0), (3, 3), (3, 2), (3, 1)),
     ((3, 3), (3, 2), (2, 2), (3, 1), (2, 1), (1, 1), (2, 0), (1, 0), (0, 0)),
 )
-THIRD, FOURTH = (2, 3, 3, 3), (4, 4, 6, 6)
+THIRD, FOURTH = (3, 3, 3, 3), (6, 4, 6, 6)
 
 
 def by_y(y, values):
@@ -125,7 +125,9 @@
     pltpu.make_async_copy(src, dst, q_recv.at[mine]).start()
     pl.semaphore_wait(barrier, 10)
 
-    others = [[2 * ((y + dy) % 4) + (xl + dx) % 2 for dx in range(2)] for dy in range(4)]
+    far = jnp.where(y == 1, 3, 2)
+    steps = (0, 1, far, 5 - far)
+    others = [[2 * ((y + dy) % 4) + (xl + dx) % 2 for dx in range(2)] for dy in steps]
     others[0] = others[0][1:]
 
     def send_kv(dy):
@@ -140,9 +142,10 @@
     send_kv(0)
     send_kv(1)
     send_kv(2)
+    send_kv(3)
 
     def key_row(i):
-        return (y + 4 - i) % 4
+        return jnp.where(y == 0, i, (y + 4 - i) % 4)
 
     def pass_on(i):
         row = key_row(i)
@@ -169,7 +172,10 @@
     pass_on(0)
     send_q(0)
     send_q(1)
-    send_kv(3)
+
+    @pl.when(y == 1)
+    def _():
+        send_q(2)
 
     starts, total = [], jnp.int32(0)
     for d in range(DOCS):
@@ -211,7 +217,11 @@
 
     pass_on(1)
     pass_on(2)
-    send_q(2)
+
+    @pl.when(y != 1)
+    def _():
+        send_q(2)
+
     send_q(3)
     receive(0)
 
@@ -312,8 +322,11 @@
 
         @pl.when(step == 1)
         def _():
+            receive(1)
+
+        @pl.when(step == 2)
+        def _():
             pass_on(3)
-            receive(1)
 
         @pl.when(step == by_y(y, THIRD))
         def _():

time: 99 us -> 95.4 us (0.964)
  Pallas kernels: 95.6 us -> 92.1 us
    pallas_call x1, Pallas kernels: 95.6 us -> 92.1 us  [on_device(): pl.pallas_call(kernel, out_shape=jax.ShapeDtypeStruct(queries.shape, bf16...]
where the time goes in v3:
time: 95.4 us; the launch traced here: 95.2 us
  Pallas kernels  92.1 us (97%)
  local copies, waits for them, and re-layouts  3.13 us (3%)
    pallas_call x1, Pallas kernels, on_device(): pl.pallas_call(kernel, out_shape=jax.ShapeDtypeStruct(queries.shape, bf16...  92.1 us
    unnamed x1, local copies, waits for them, and re-layouts  3.13 us

profile of v3, /device:TPU:17, one launch (start us, length us, event | category | flops | bytes accessed | tf_op | source)
XLA Modules:
  0.0 95.2 jit_solution(11678919652276317433)
XLA Ops:
  0.0 92.1 %shard_map.46 = bf16[256,4096]{1,0:T(8,128)(2,1)} custom-call(s32[6]{0:T(128)} %lengths.1, bf16[256,4096]{1,0:T(8,128)(2,1)} %q_hbm.1, bf16[256,1024]{1,0:T(8,128)(2,1)} %k_hbm.1, bf16[256,1024]{1,0:T(8,128)(2,1)} %v_hbm.1), custom_call_target="tpu_custom_call" | custom-call | tf_op jit(solution)/shard_map/pallas_call | solution.py:390
  92.1 3.1 %copy.6 = bf16[256,4096]{1,0:T(8,128)(2,1)} copy(bf16[256,4096]{1,0:T(8,128)(2,1)} %shard_map.46) | data formatting | bytes 4194304

commit v4 on v3

--- a/solution.py
+++ b/solution.py
@@ -218,11 +218,14 @@
     pass_on(1)
     pass_on(2)
 
-    @pl.when(y != 1)
+    @pl.when((y == 0) | (y == 3))
     def _():
         send_q(2)
 
-    send_q(3)
+    @pl.when(y != 2)
+    def _():
+        send_q(3)
+
     receive(0)
 
     def scores(r, t, u, c, mx, qoff=None):
@@ -322,6 +325,11 @@
 
         @pl.when(step == 1)
         def _():
+            @pl.when(y == 2)
+            def _():
+                send_q(2)
+                send_q(3)
+
             receive(1)
 
         @pl.when(step == 2)

time: 95.4 us -> 95.4 us (level)
  no operation moved by 1% of the time
where the time goes in v4:
time: 95.4 us; the launch traced here: 95.2 us
  Pallas kernels  92.1 us (97%)
  local copies, waits for them, and re-layouts  3.13 us (3%)
    pallas_call x1, Pallas kernels, on_device(): pl.pallas_call(kernel, out_shape=jax.ShapeDtypeStruct(queries.shape, bf16...  92.1 us
    unnamed x1, local copies, waits for them, and re-layouts  3.13 us

profile of v4, /device:TPU:17, one launch (start us, length us, event | category | flops | bytes accessed | tf_op | source)
XLA Modules:
  0.0 95.2 jit_solution(5874356361665825609)
XLA Ops:
  0.0 92.1 %shard_map.46 = bf16[256,4096]{1,0:T(8,128)(2,1)} custom-call(s32[6]{0:T(128)} %lengths.1, bf16[256,4096]{1,0:T(8,128)(2,1)} %q_hbm.1, bf16[256,1024]{1,0:T(8,128)(2,1)} %k_hbm.1, bf16[256,1024]{1,0:T(8,128)(2,1)} %v_hbm.1), custom_call_target="tpu_custom_call" | custom-call | tf_op jit(solution)/shard_map/pallas_call | solution.py:398
  92.1 3.1 %copy.6 = bf16[256,4096]{1,0:T(8,128)(2,1)} copy(bf16[256,4096]{1,0:T(8,128)(2,1)} %shard_map.46) | data formatting | bytes 4194304
